TPU v7x, 512 devices: a whole 4x4x16 slice. The times are simulated.
512 devices in a mesh: gx: 32 (over z, core), gy: 16 (over y, x).
Axes of the slice: x: 4, y: 4, z: 16, core: 2. Of those that a mesh axis runs over, the one named last changes fastest.
Arguments:
- bin_state: float32 [132, 256, 2048], P(None, 'gx', 'gy'), may hold values from 0.05 to 2
- courant_x: float32 [256, 2048], P('gx', 'gy'), may hold values from -0.4 to 0.4
- courant_y: float32 [256, 2048], P('gx', 'gy'), may hold values from -0.4 to 0.4
- cloudy_order: int32 [32, 16, 8], P('gx', 'gy'), may hold values from 0 to 7, each once within a row
- block_count: int32 [16, 32], P('gy', 'gx'), may hold values from 1 to 8, 160 in all within a row
- gain_kernel: bfloat16 [10, 33, 1089], replicated, may hold values from -0.059814453 to 0.059814453
- loss_rate: bfloat16 [10, 33, 33], replicated, may hold values from 9.9658966e-05 to 0.029907227
Outputs:
- state_out: float32 [132, 256, 2048], P(None, 'gx', 'gy')
Inputs may be any that keep to these rules, and one draw needn't show every extreme that they name: `cloudy_order`: each device's row holds each of its 8 block numbers once. `block_count`: each row of 32 counts sums to 160, and its largest count is 8.
All inputs are finite; a program needn't handle non-finite values. No bound on the sum of `block_count` on one device may be relied on, other than what follows from the above.
Results may differ from a plain program's by a relative error of at most 0.0034.
Values may be sent and summed in bfloat16 or wider, within the bound.
A program may use at most 128 MiB of HBM per device.

v0:
```python
import jax
import jax.numpy as jnp
from jax import lax
from jax.sharding import PartitionSpec as P

BINS = 33
CLASSES = 4
LEV = 4
STEPS = 2


pair_table = (
    (0, 0, 1),
    (0, 1, 1),
    (0, 2, 2),
    (0, 3, 3),
    (1, 1, 1),
    (1, 2, 3),
    (1, 3, 3),
    (2, 2, 3),
    (2, 3, 3),
    (3, 3, 3),
)


def with_halo(shard, sides, width):
    for axis, dim in sides:
        size, length = (lax.axis_size(axis), shard.shape[dim])
        up = [(i, (i + 1) % size) for i in range(size)]
        down = [(j, i) for i, j in up]
        last = lax.slice_in_dim(shard, length - width, length, axis=dim)
        leading = lax.slice_in_dim(shard, 0, width, axis=dim)
        before = lax.ppermute(last, axis, up)
        after = lax.ppermute(leading, axis, down)
        shard = jnp.concatenate([before, shard, after], axis=dim)
    return shard


def upwind(centre, minus_one, minus_two, plus_one, plus_two, courant):
    rising = (2.0 * plus_one + 3.0 * centre - 6.0 * minus_one + minus_two) / 6.0
    falling = (6.0 * plus_one - plus_two - 3.0 * centre - 2.0 * minus_one) / 6.0
    return jnp.where(courant > 0.0, rising, falling)


def transport(fields, courant_x, courant_y):
    wide_x = with_halo(fields.astype(jnp.bfloat16), (("gx", 1),), 2).astype(fields.dtype)
    along_x = upwind(
        fields, wide_x[:, 1:-3], wide_x[:, :-4], wide_x[:, 3:-1], wide_x[:, 4:], courant_x[None]
    )
    wide_y = with_halo(fields.astype(jnp.bfloat16), (("gy", 2),), 2 * LEV).astype(fields.dtype)
    along_y = upwind(
        fields,
        wide_y[:, :, LEV : -3 * LEV],
        wide_y[:, :, : -4 * LEV],
        wide_y[:, :, 3 * LEV : -LEV],
        wide_y[:, :, 4 * LEV :],
        courant_y[None],
    )
    return jnp.maximum(fields - courant_x[None] * along_x - courant_y[None] * along_y, 0.0)


def collide(bin_values, gain_kernel, loss_rate):
    column_count = bin_values.shape[1]
    tendency = [jnp.zeros((BINS, column_count), jnp.float32) for member in range(CLASSES)]
    for pair_index, (former, latter, target) in enumerate(pair_table):
        former_bins = bin_values[former * BINS : (former + 1) * BINS]
        latter_bins = bin_values[latter * BINS : (latter + 1) * BINS]
        product = (former_bins[:, None, :] * latter_bins[None, :, :]).reshape(
            BINS * BINS, column_count
        )
        tendency[target] = tendency[target] + jnp.dot(
            gain_kernel[pair_index], product, preferred_element_type=jnp.float32
        )
        tendency[former] = tendency[former] - former_bins.astype(jnp.float32) * jnp.dot(
            loss_rate[pair_index], latter_bins, preferred_element_type=jnp.float32
        )
        tendency[latter] = tendency[latter] - latter_bins.astype(jnp.float32) * jnp.dot(
            loss_rate[pair_index].T, former_bins, preferred_element_type=jnp.float32
        )
    return jnp.concatenate(tendency, axis=0)


def per_device(bin_state, courant_x, courant_y, cloudy_order, block_count, gain_kernel, loss_rate):
    state_now = bin_state
    block_rows = state_now.shape[1]
    block_order = cloudy_order[0, 0]
    own_count = block_count[0, 0]
    row_numbers = jnp.arange(block_rows, dtype=jnp.int32)
    matches = (block_order[:, None] == row_numbers[None, :]).astype(jnp.int32)
    position = jnp.sum(matches * row_numbers[:, None], axis=0)
    cloudy = position < own_count
    for step_index in range(STEPS):
        state_now = transport(state_now, courant_x, courant_y)
        bin_values = state_now.astype(jnp.bfloat16)
        shaped = bin_values.shape
        gained = collide(
            bin_values.reshape(shaped[0], shaped[1] * shaped[2]), gain_kernel, loss_rate
        )
        gained = gained.astype(jnp.bfloat16).reshape(shaped)
        tendency = jnp.where(cloudy[None, :, None], gained, jnp.zeros((), jnp.bfloat16))
        state_now = state_now + tendency.astype(jnp.float32)
    return state_now


def solution(mesh):
    placed = (
        P(None, "gx", "gy"),
        P("gx", "gy"),
        P("gx", "gy"),
        P("gx", "gy", None),
        P("gy", "gx"),
        P(),
        P(),
    )
    return jax.shard_map(
        per_device, mesh=mesh, in_specs=placed, out_specs=P(None, "gx", "gy"), check_vma=False
    )
```

profile of v0, /device:TPU:2, one launch (start us, length us, event | category | flops | bytes accessed | tf_op | source)
XLA Modules:
  0.0 200.1 jit_solution(2512257483897506616)
XLA Ops:
  1.3 7.9 %collective-permute-start.3 = (bf16[132,8,8]{2,1,0:T(8,128)(2,1)S(1)}, bf16[132,8,8]{2,1,0:T(8,128)(2,1)S(1)}, u32[]{:S(2)}, u32[]{:S(2)}) collective-permute-start(bf16[132,8,8]{2,1,0:T(8,128)(2,1)S(1)} %get-tuple-element.24), channel_id=1, source_target_pairs={{1,0},{2,1},{3,2},{4,3},{5,4},{6,5},{7,6},{8,7},{9,8},{10,9},{11,1... | collective-permute-start | bytes 50696 | tf_op jit(solution)/shard_map/ppermute | solution.py:34
  11.2 4.5 %collective-permute-start.1 = (bf16[132,2,128]{2,1,0:T(2,128)(2,1)S(1)}, bf16[132,2,128]{2,1,0:T(2,128)(2,1)S(1)}, u32[]{:S(2)}, u32[]{:S(2)}) collective-permute-start(bf16[132,2,128]{2,1,0:T(2,128)(2,1)S(1)} %get-tuple-element.22), channel_id=1, source_target_pairs={{16,0},{32,16},{48,32},{64,48},{80,64},{96,80},{112,96},{128,112},... | collective-permute-start | bytes 202760 | tf_op jit(solution)/shard_map/ppermute | solution.py:34
  22.7 8.2 %broadcast_multiply_fusion.18 = (bf16[33,33,1024]{2,1,0:T(8,128)(2,1)}, bf16[33,33,1024]{2,1,0:T(8,128)(2,1)}, bf16[33,33,1024]{2,1,0:T(8,128)(2,1)}, bf16[33,33...) fusion(bf16[33,1024]{1,0:T(8,128)(2,1)S(1)} %bitcast.612, ...), kind=kLoop, calls=%fused_computation.18 | loop fusion | flops 11151360 | bytes 22573056 | tf_op jit(solution)/shard_map/mul | solution.py:68
  31.0 4.6 %mul.688 = bf16[1089,1024]{1,0:T(8,128)(2,1)} reshape(bf16[33,33,1024]{2,1,0:T(8,128)(2,1)} %get-tuple-element.41) | data formatting | bytes 4460544 | tf_op jit(solution)/shard_map/mul | solution.py:68
  35.6 4.6 %mul.684 = bf16[1089,1024]{1,0:T(8,128)(2,1)} reshape(bf16[33,33,1024]{2,1,0:T(8,128)(2,1)} %get-tuple-element.38) | data formatting | bytes 4460544 | tf_op jit(solution)/shard_map/mul | solution.py:68
  44.5 4.6 %mul.682 = bf16[1089,1024]{1,0:T(8,128)(2,1)} reshape(bf16[33,33,1024]{2,1,0:T(8,128)(2,1)} %get-tuple-element.42) | data formatting | bytes 4460544 | tf_op jit(solution)/shard_map/mul | solution.py:68
  51.3 4.6 %mul.678 = bf16[1089,1024]{1,0:T(8,128)(2,1)} reshape(bf16[33,33,1024]{2,1,0:T(8,128)(2,1)} %get-tuple-element.40) | data formatting | bytes 4460544 | tf_op jit(solution)/shard_map/mul | solution.py:68
  58.7 4.6 %mul.676 = bf16[1089,1024]{1,0:T(8,128)(2,1)} reshape(bf16[33,33,1024]{2,1,0:T(8,128)(2,1)} %get-tuple-element.37) | data formatting | bytes 4460544 | tf_op jit(solution)/shard_map/mul | solution.py:68
  66.0 4.6 %mul.673 = bf16[1089,1024]{1,0:T(8,128)(2,1)} reshape(bf16[33,33,1024]{2,1,0:T(8,128)(2,1)} %get-tuple-element.39) | data formatting | bytes 4460544 | tf_op jit(solution)/shard_map/mul | solution.py:68
  74.8 4.6 %mul.665 = bf16[1089,1024]{1,0:T(8,128)(2,1)} reshape(bf16[33,33,1024]{2,1,0:T(8,128)(2,1)} %get-tuple-element.36) | data formatting | bytes 4460544 | tf_op jit(solution)/shard_map/mul | solution.py:68
  82.5 4.6 %mul.658 = bf16[1089,1024]{1,0:T(8,128)(2,1)} reshape(bf16[33,33,1024]{2,1,0:T(8,128)(2,1)} %get-tuple-element.44) | data formatting | bytes 4460544 | tf_op jit(solution)/shard_map/mul | solution.py:68
  93.5 3.5 %mul.654 = bf16[1089,1024]{1,0:T(8,128)(2,1)S(1)} reshape(bf16[33,33,1024]{2,1,0:T(8,128)(2,1)} %get-tuple-element.35) | data formatting | bytes 4460544 | tf_op jit(solution)/shard_map/mul | solution.py:68
  100.4 5.9 %collective-permute-start.7 = (bf16[132,8,8]{2,1,0:T(8,128)(2,1)S(1)}, bf16[132,8,8]{2,1,0:T(8,128)(2,1)S(1)}, u32[]{:S(2)}, u32[]{:S(2)}) collective-permute-start(bf16[132,8,8]{2,1,0:T(8,128)(2,1)S(1)} %get-tuple-element.16), channel_id=1, source_target_pairs={{1,0},{2,1},{3,2},{4,3},{5,4},{6,5},{7,6},{8,7},{9,8},{10,9},{11,1... | collective-permute-start | bytes 50696 | tf_op jit(solution)/shard_map/ppermute | solution.py:34
  108.5 5.4 %collective-permute-start.5 = (bf16[132,2,128]{2,1,0:T(2,128)(2,1)S(1)}, bf16[132,2,128]{2,1,0:T(2,128)(2,1)S(1)}, u32[]{:S(2)}, u32[]{:S(2)}) collective-permute-start(bf16[132,2,128]{2,1,0:T(2,128)(2,1)S(1)} %get-tuple-element.14), channel_id=1, source_target_pairs={{16,0},{32,16},{48,32},{64,48},{80,64},{96,80},{112,96},{128,112},... | collective-permute-start | bytes 202760 | tf_op jit(solution)/shard_map/ppermute | solution.py:34
  113.9 3.8 %collective-permute-done.6 = bf16[132,8,8]{2,1,0:T(8,128)(2,1)S(1)} collective-permute-done((bf16[132,8,8]{2,1,0:T(8,128)(2,1)S(1)}, bf16[132,8,8]{2,1,0:T(8,128)(2,1)S(1)}, u32[]{:S(2)}, u32[]{:S(2)}) %collective-permute-start.6) | collective-permute-done | bytes 16928 | tf_op jit(solution)/shard_map/ppermute | solution.py:33
  122.1 8.2 %broadcast_multiply_fusion.8 = (bf16[33,33,1024]{2,1,0:T(8,128)(2,1)}, bf16[33,33,1024]{2,1,0:T(8,128)(2,1)}, bf16[33,33,1024]{2,1,0:T(8,128)(2,1)}, bf16[33,33,...) fusion(bf16[33,1024]{1,0:T(8,128)(2,1)S(1)} %bitcast.603, ...), kind=kLoop, calls=%fused_computation.8 | loop fusion | flops 11151360 | bytes 22573056 | tf_op jit(solution)/shard_map/mul | solution.py:68
  130.3 4.6 %mul.747 = bf16[1089,1024]{1,0:T(8,128)(2,1)} reshape(bf16[33,33,1024]{2,1,0:T(8,128)(2,1)} %get-tuple-element.31) | data formatting | bytes 4460544 | tf_op jit(solution)/shard_map/mul | solution.py:68
  137.7 4.6 %mul.743 = bf16[1089,1024]{1,0:T(8,128)(2,1)} reshape(bf16[33,33,1024]{2,1,0:T(8,128)(2,1)} %get-tuple-element.28) | data formatting | bytes 4460544 | tf_op jit(solution)/shard_map/mul | solution.py:68
  144.4 4.6 %mul.741 = bf16[1089,1024]{1,0:T(8,128)(2,1)} reshape(bf16[33,33,1024]{2,1,0:T(8,128)(2,1)} %get-tuple-element.32) | data formatting | bytes 4460544 | tf_op jit(solution)/shard_map/mul | solution.py:68
  151.1 4.6 %mul.737 = bf16[1089,1024]{1,0:T(8,128)(2,1)} reshape(bf16[33,33,1024]{2,1,0:T(8,128)(2,1)} %get-tuple-element.30) | data formatting | bytes 4460544 | tf_op jit(solution)/shard_map/mul | solution.py:68
  158.5 4.6 %mul.735 = bf16[1089,1024]{1,0:T(8,128)(2,1)} reshape(bf16[33,33,1024]{2,1,0:T(8,128)(2,1)} %get-tuple-element.27) | data formatting | bytes 4460544 | tf_op jit(solution)/shard_map/mul | solution.py:68
  165.9 4.6 %mul.732 = bf16[1089,1024]{1,0:T(8,128)(2,1)} reshape(bf16[33,33,1024]{2,1,0:T(8,128)(2,1)} %get-tuple-element.29) | data formatting | bytes 4460544 | tf_op jit(solution)/shard_map/mul | solution.py:68
  173.8 4.6 %mul.724 = bf16[1089,1024]{1,0:T(8,128)(2,1)} reshape(bf16[33,33,1024]{2,1,0:T(8,128)(2,1)} %get-tuple-element.26) | data formatting | bytes 4460544 | tf_op jit(solution)/shard_map/mul | solution.py:68
  181.6 4.6 %mul.717 = bf16[1089,1024]{1,0:T(8,128)(2,1)} reshape(bf16[33,33,1024]{2,1,0:T(8,128)(2,1)} %get-tuple-element.34) | data formatting | bytes 4460544 | tf_op jit(solution)/shard_map/mul | solution.py:68
  (154 shorter events, 77.6 us)
Async XLA Ops:
  1.1 19.9 %copy-start.3 = (f32[132,8,128]{2,1,0:T(8,128)S(1)}, f32[132,8,128]{2,1,0:T(8,128)}, u32[]{:S(2)}) copy-start(f32[132,8,128]{2,1,0:T(8,128)} %param.7) | copy-start | bytes 1622020
  1.1 19.9 %copy-start.13 = (f32[8,128]{1,0:T(8,128)S(1)}, f32[8,128]{1,0:T(8,128)}, u32[]{:S(2)}) copy-start(f32[8,128]{1,0:T(8,128)} %param.9) | copy-start | bytes 12292
  1.1 19.9 %copy-start.14 = (f32[8,128]{1,0:T(8,128)S(1)}, f32[8,128]{1,0:T(8,128)}, u32[]{:S(2)}) copy-start(f32[8,128]{1,0:T(8,128)} %param.8) | copy-start | bytes 12292
  1.3 16.6 %collective-permute-start.3 = (bf16[132,8,8]{2,1,0:T(8,128)(2,1)S(1)}, bf16[132,8,8]{2,1,0:T(8,128)(2,1)S(1)}, u32[]{:S(2)}, u32[]{:S(2)}) collective-permute-start(bf16[132,8,8]{2,1,0:T(8,128)(2,1)S(1)} %get-tuple-element.24), channel_id=1, source_target_pairs={{1,0},{2,1},{3,2},{4,3},{5,4},{6,5},{7,6},{8,7},{9,8},{10,9},{11,1... | collective-permute-start | bytes 50696 | tf_op jit(solution)/shard_map/ppermute | solution.py:34
  9.2 8.7 %collective-permute-start.2 = (bf16[132,8,8]{2,1,0:T(8,128)(2,1)S(1)}, bf16[132,8,8]{2,1,0:T(8,128)(2,1)S(1)}, u32[]{:S(2)}, u32[]{:S(2)}) collective-permute-start(bf16[132,8,8]{2,1,0:T(8,128)(2,1)S(1)} %get-tuple-element.23), channel_id=1, source_target_pairs={{0,1},{1,2},{2,3},{3,4},{4,5},{5,6},{6,7},{7,8},{8,9},{9,10},{10,1... | collective-permute-start | bytes 50696 | tf_op jit(solution)/shard_map/ppermute | solution.py:33
  11.2 7.0 %collective-permute-start.1 = (bf16[132,2,128]{2,1,0:T(2,128)(2,1)S(1)}, bf16[132,2,128]{2,1,0:T(2,128)(2,1)S(1)}, u32[]{:S(2)}, u32[]{:S(2)}) collective-permute-start(bf16[132,2,128]{2,1,0:T(2,128)(2,1)S(1)} %get-tuple-element.22), channel_id=1, source_target_pairs={{16,0},{32,16},{48,32},{64,48},{80,64},{96,80},{112,96},{128,112},... | collective-permute-start | bytes 202760 | tf_op jit(solution)/shard_map/ppermute | solution.py:34
  15.7 4.9 %collective-permute-start = (bf16[132,2,128]{2,1,0:T(2,128)(2,1)S(1)}, bf16[132,2,128]{2,1,0:T(2,128)(2,1)S(1)}, u32[]{:S(2)}, u32[]{:S(2)}) collective-permute-start(bf16[132,2,128]{2,1,0:T(2,128)(2,1)S(1)} %get-tuple-element.21), channel_id=1, source_target_pairs={{0,16},{16,32},{32,48},{48,64},{64,80},{80,96},{96,112},{112,128},... | collective-permute-start | bytes 202760 | tf_op jit(solution)/shard_map/ppermute | solution.py:33
  40.2 3.0 %copy-start = (bf16[1089,1024]{1,0:T(8,128)(2,1)S(1)}, bf16[1089,1024]{1,0:T(8,128)(2,1)}, u32[]{:S(2)}) copy-start(bf16[1089,1024]{1,0:T(8,128)(2,1)} %mul.684) | copy-start | bytes 6690820
  70.6 2.2 %copy-start.4 = (bf16[10,33,33]{2,1,0:T(8,128)(2,1)S(1)}, bf16[10,33,33]{2,1,0:T(8,128)(2,1)}, u32[]{:S(2)}) copy-start(bf16[10,33,33]{2,1,0:T(8,128)(2,1)} %param.13) | copy-start | bytes 65344
  70.6 3.0 %copy-start.5 = (f32[33,1024]{1,0:T(8,128)S(1)}, f32[33,1024]{1,0:T(8,128)}, u32[]{:S(2)}) copy-start(f32[33,1024]{1,0:T(8,128)} %convolution_bitcast_fusion.51) | copy-start | bytes 405508
  70.6 3.1 %copy-start.7 = (f32[33,1024]{1,0:T(8,128)S(1)}, f32[33,1024]{1,0:T(8,128)}, u32[]{:S(2)}) copy-start(f32[33,1024]{1,0:T(8,128)} %convolution_bitcast_fusion.52) | copy-start | bytes 405508
  70.7 3.5 %copy-start.10 = (f32[33,1024]{1,0:T(8,128)S(1)}, f32[33,1024]{1,0:T(8,128)}, u32[]{:S(2)}) copy-start(f32[33,1024]{1,0:T(8,128)} %convolution_bitcast_fusion.48) | copy-start | bytes 405508
  98.4 1.0 copy-start.12
  98.6 1.5 copy-start.1
  100.4 13.6 %collective-permute-start.7 = (bf16[132,8,8]{2,1,0:T(8,128)(2,1)S(1)}, bf16[132,8,8]{2,1,0:T(8,128)(2,1)S(1)}, u32[]{:S(2)}, u32[]{:S(2)}) collective-permute-start(bf16[132,8,8]{2,1,0:T(8,128)(2,1)S(1)} %get-tuple-element.16), channel_id=1, source_target_pairs={{1,0},{2,1},{3,2},{4,3},{5,4},{6,5},{7,6},{8,7},{9,8},{10,9},{11,1... | collective-permute-start | bytes 50696 | tf_op jit(solution)/shard_map/ppermute | solution.py:34
  106.3 11.4 %collective-permute-start.6 = (bf16[132,8,8]{2,1,0:T(8,128)(2,1)S(1)}, bf16[132,8,8]{2,1,0:T(8,128)(2,1)S(1)}, u32[]{:S(2)}, u32[]{:S(2)}) collective-permute-start(bf16[132,8,8]{2,1,0:T(8,128)(2,1)S(1)} %get-tuple-element.15), channel_id=1, source_target_pairs={{0,1},{1,2},{2,3},{3,4},{4,5},{5,6},{6,7},{7,8},{8,9},{9,10},{10,1... | collective-permute-start | bytes 50696 | tf_op jit(solution)/shard_map/ppermute | solution.py:33
  108.5 9.5 %collective-permute-start.5 = (bf16[132,2,128]{2,1,0:T(2,128)(2,1)S(1)}, bf16[132,2,128]{2,1,0:T(2,128)(2,1)S(1)}, u32[]{:S(2)}, u32[]{:S(2)}) collective-permute-start(bf16[132,2,128]{2,1,0:T(2,128)(2,1)S(1)} %get-tuple-element.14), channel_id=1, source_target_pairs={{16,0},{32,16},{48,32},{64,48},{80,64},{96,80},{112,96},{128,112},... | collective-permute-start | bytes 202760 | tf_op jit(solution)/shard_map/ppermute | solution.py:34
  113.9 4.9 %collective-permute-start.4 = (bf16[132,2,128]{2,1,0:T(2,128)(2,1)S(1)}, bf16[132,2,128]{2,1,0:T(2,128)(2,1)S(1)}, u32[]{:S(2)}, u32[]{:S(2)}) collective-permute-start(bf16[132,2,128]{2,1,0:T(2,128)(2,1)S(1)} %get-tuple-element.13), channel_id=1, source_target_pairs={{0,16},{16,32},{32,48},{48,64},{64,80},{80,96},{96,112},{112,128},... | collective-permute-start | bytes 202760 | tf_op jit(solution)/shard_map/ppermute | solution.py:33
  170.5 2.2 %copy-start.6 = (f32[33,1024]{1,0:T(8,128)S(1)}, f32[33,1024]{1,0:T(8,128)}, u32[]{:S(2)}) copy-start(f32[33,1024]{1,0:T(8,128)} %convolution_bitcast_fusion.43) | copy-start | bytes 405508
  170.5 2.2 %copy-start.8 = (f32[33,1024]{1,0:T(8,128)S(1)}, f32[33,1024]{1,0:T(8,128)}, u32[]{:S(2)}) copy-start(f32[33,1024]{1,0:T(8,128)} %convolution_bitcast_fusion.44) | copy-start | bytes 405508
  170.5 2.7 %copy-start.9 = (f32[33,1024]{1,0:T(8,128)S(1)}, f32[33,1024]{1,0:T(8,128)}, u32[]{:S(2)}) copy-start(f32[33,1024]{1,0:T(8,128)} %convolution_bitcast_fusion.40) | copy-start | bytes 405508
  197.5 1.0 copy-start.11
  197.7 1.5 copy-start.2
where the time goes:
time: 203 us; the launch traced here: 200 us
  local copies, waits for them, and re-layouts  85.8 us (42%)
  matrix products  53.3 us (26%)
  starting transfers between devices  27.8 us (14%)
  other arithmetic  24.7 us (12%)
  waiting for transfers between devices  7.05 us (3%)
    mul x20, local copies, waits for them, and re-layouts, collide(): former_bins[:, None, :] * latter_bins[None, :, :]  84.9 us
    dot_general x20, matrix products, collide(): jnp.dot(gain_kernel[pair_index], product, preferred_element_type=jnp.floa...  44.6 us
    ppermute x4, starting transfers between devices, with_halo(): after = lax.ppermute(leading, axis, down)  23.8 us
    mul x2, other arithmetic, collide(): former_bins[:, None, :] * latter_bins[None, :, :]  16.4 us
    ppermute x4, waiting for transfers between devices, with_halo(): before = lax.ppermute(last, axis, up)  7.04 us
    dot_general x20, matrix products, collide(): jnp.dot(loss_rate[pair_index], latter_bins, preferred_element_type=jnp.fl...  4.44 us
    dot_general x20, matrix products, collide(): jnp.dot(loss_rate[pair_index].T, former_bins, preferred_element_type=jnp....  4.29 us
  transfers between devices with their start and end apart: 8, of which 3 were waited for; matrix products, arithmetic and copies ran while one was open for 1% of the time, Pallas kernels for 0%

commit v1 on v0

v1 whole, which is shorter than its diff:
```python
import jax
import jax.numpy as jnp
import numpy as np
from jax import lax
from jax.experimental import pallas as pl
from jax.experimental.pallas import tpu as pltpu
from jax.sharding import PartitionSpec as P

BINS = 33
COMPS = 132
ROWS = 136
PACKED = 144
LEV = 4
CX = 8
LANES = 128
HALF = 512
FLAT = BINS * BINS
WIDE = 1152
MESH = pl.DeviceIdType.MESH
F32, BF16 = jnp.float32, jnp.bfloat16

OFFSET = (0, 33, 66, 128)
STACK = (3, 6, 8, 5, 0, 1, 2, 4, 7, 9)
SWAPPED = 4
PLACE = {p: s for s, p in enumerate(STACK)}
GROUPS = (
    (1, 0, ((0, 0), (1, 1))),
    (1, 1, ((4, 1),)),
    (2, 0, ((2, 2),)),
    (3, 2, ((5, 1), (7, 2))),
    (3, 3, ((3, 0), (6, 1), (8, 2), (9, 3))),
)
PAIR_OF = {(0, 0): 0, (0, 1): 1, (0, 2): 2, (0, 3): 3, (1, 1): 4, (1, 2): 5, (1, 3): 6, (2, 2): 7, (2, 3): 8, (3, 3): 9}
CHUNK = 11
SLAB = BINS * 32


def iota(shape, dim):
    return lax.broadcasted_iota(jnp.int32, shape, dim)


def stack_gain(gain, stacked):
    stacked[...] = jnp.zeros_like(stacked)
    for place, pair in enumerate(STACK):
        stacked[place * 48 : place * 48 + BINS, 0:FLAT] = gain[pair]


def exchange(stacked, chooser):
    rows = SWAPPED * 48
    source = stacked[0:rows, :]
    width = 384
    parts = []
    for part in range(WIDE // width):
        column = iota((1, width), 1) + part * width
        high = (column * 1986) >> 16
        origin = jnp.where(column < FLAT, (column - high * BINS) * BINS + high, -1)
        chooser[...] = jnp.where(iota((WIDE, width), 0) == origin, 1.0, 0.0).astype(BF16)
        parts.append(
            jnp.dot(source, chooser[...], preferred_element_type=F32).astype(BF16)
        )
    for part in range(WIDE // width):
        stacked[0:rows, part * width : (part + 1) * width] = parts[part]


def window(stacked, pair, index, lane0):
    row = PLACE[pair] * 48
    start = index * BINS
    tile, off = start // LANES, start % LANES
    shift = (lane0 - off) % LANES
    def moved(t):
        value = stacked[row : row + 48, t * LANES : (t + 1) * LANES]
        return pltpu.roll(value, shift, 1) if shift else value
    first = moved(tile)
    if off + BINS <= LANES:
        return first
    return jnp.where(iota((48, LANES), 1) < lane0 + LANES - off, first, moved(tile + 1))


def build_gain(stacked, matrix, corner, corner2):
    lane = iota((48, LANES), 1)
    corner[...] = jnp.zeros_like(corner)
    corner2[...] = jnp.zeros_like(corner2)
    for group, (target, factor, pairs) in enumerate(GROUPS):
        for index in range(BINS):
            low, high = None, None
            for pair, cls in sorted(pairs, key=lambda entry: entry[1]):
                lane0 = OFFSET[cls] % LANES
                piece = window(stacked, pair, index, lane0)
                inside = (lane >= lane0) & (lane < lane0 + BINS)
                if cls == 3:
                    high = jnp.where(inside, piece, jnp.zeros_like(piece))
                else:
                    low = jnp.where(inside, piece, jnp.zeros_like(piece) if low is None else low)
            row = group * SLAB + index * 32
            for value, col in ((low, 0), (high, LANES)):
                if value is None:
                    continue
                matrix[row : row + 32, col : col + LANES] = value[0:32]
                last = value[32:48].astype(F32)[0:1]
                if target == 2:
                    corner2[index : index + 1, :] = last
                else:
                    at = factor * BINS + index
                    corner[at : at + 1, col : col + LANES] = last


def build_loss(loss, square, table):
    table[...] = jnp.zeros_like(table)
    square[...] = jnp.zeros_like(square)
    for (a, b), pair in PAIR_OF.items():
        square[0:BINS, 0:BINS] = loss[pair].astype(F32)
        plain = square[...]
        turned = plain.T
        if a == b:
            plain = plain + turned
        table[a * BINS : a * BINS + BINS, OFFSET[b] : OFFSET[b] + BINS] = plain[0:BINS, 0:BINS]
        if a != b:
            table[b * BINS : b * BINS + BINS, OFFSET[a] : OFFSET[a] + BINS] = turned[0:BINS, 0:BINS]


def build_weights(cx, cy, weights):
    own = jnp.ones((CX, LANES), F32)
    for axis, ref in enumerate((cx, cy)):
        c = ref[...]
        up = c > 0.0
        weights[axis * 4 + 0] = c * jnp.where(up, 1.0 / 3.0, 1.0)
        weights[axis * 4 + 1] = c * jnp.where(up, 0.0, -1.0 / 6.0)
        weights[axis * 4 + 2] = c * jnp.where(up, -1.0, -1.0 / 3.0)
        weights[axis * 4 + 3] = c * jnp.where(up, 1.0 / 6.0, 0.0)
        own = own - c * jnp.where(up, 0.5, -0.5)
    weights[8] = own


def pack_y(wide, ys):
    ys[...] = jnp.zeros_like(ys)
    for row in range(0, ROWS, 16):
        n = min(16, ROWS - row)
        lane = iota((n, LANES), 1)
        left = jnp.zeros((n, LANES), F32)
        right = jnp.zeros((n, LANES), F32)
        for b in range(CX):
            value = wide[b + 2, row : row + n, :]
            inside = (lane >= 8 * b) & (lane < 8 * b + 8)
            left = jnp.where(inside, pltpu.roll(value, 8 * b, 1) if b else value, left)
            right = jnp.where(inside, pltpu.roll(value, (8 * b + 8) % LANES, 1), right)
        ys[0, row : row + n, :] = left.astype(BF16)
        ys[1, row : row + n, :] = right.astype(BF16)


def transport(wide, left, right, weights, moved, cells, cells16):
    def block(pos, carry):
        b = (pos + 6) % 8
        half, col = pos // 4, pl.multiple_of((pos % 4) * LANES, LANES)
        w = [weights[k, pl.ds(b, 1), :] for k in range(9)]
        back = (120 - 8 * b) % LANES
        fore = (LANES - 8 * b) % LANES
        for row in range(0, ROWS, 16):
            n = min(16, ROWS - row)
            lane = iota((n, LANES), 1)
            rows = slice(row, row + n)
            q = wide[b + 2, rows, :]
            total = w[8] * q
            total = total - w[0] * wide[b + 3, rows, :] - w[1] * wide[b + 4, rows, :]
            total = total - w[2] * wide[b + 1, rows, :] - w[3] * wide[b, rows, :]
            before = pltpu.roll(left[rows, :].astype(F32), back, 1)
            after = pltpu.roll(right[rows, :].astype(F32), fore, 1)
            total = total - w[4] * pltpu.roll(jnp.where(lane < LEV, after, q), LANES - LEV, 1)
            total = total - w[5] * pltpu.roll(jnp.where(lane < 2 * LEV, after, q), LANES - 2 * LEV, 1)
            total = total - w[6] * pltpu.roll(jnp.where(lane >= LANES - LEV, before, q), LEV, 1)
            total = total - w[7] * pltpu.roll(jnp.where(lane >= LANES - 2 * LEV, before, q), 2 * LEV, 1)
            total = jnp.maximum(total, 0.0)
            moved[b, rows, :] = total
            rounded = total.astype(BF16)
            cells[half, rows, pl.ds(col, LANES)] = rounded.astype(F32)
            if row < 96:
                cells16[half, rows, pl.ds(col, LANES)] = rounded
            elif row == 96:
                kept = jnp.where(iota((n, LANES), 0) < 3, total, 0.0)
                cells16[half, rows, pl.ds(col, LANES)] = kept.astype(BF16)
        cells16[half, 128:176, pl.ds(col, LANES)] = cells[half, 99:147, pl.ds(col, LANES)].astype(BF16)
        return carry

    lax.fori_loop(0, CX, block, 0)


def collide(half, matrix, corner16, table16, moved, cells, cells16, gained, cloudy, put):
    total = {}
    for group, (target, factor, pairs) in enumerate(GROUPS):
        depth = 256 if any(cls == 3 for _, cls in pairs) else 128
        for first in range(0, BINS, CHUNK):
            row = group * SLAB + first * 32
            part = jnp.dot(
                matrix[row : row + CHUNK * 32, 0:depth],
                cells16[half, 0:depth, :],
                preferred_element_type=F32,
            )
            for k in range(CHUNK):
                at = factor * BINS + first + k
                term = cells[half, at : at + 1, :] * part[32 * k : 32 * k + 32]
                total[target] = total[target] + term if target in total else term
    for target in (1, 2, 3):
        gained[target * BINS : target * BINS + 32, :] = total[target]
    last = jnp.dot(corner16[...], cells16[half], preferred_element_type=F32)
    ends = last[0:ROWS] * cells[half, 0:ROWS, :]
    below = iota((ROWS, HALF), 0) < 2 * BINS
    gained[65:66, :] = jnp.sum(jnp.where(below, ends, 0.0), axis=0, keepdims=True)
    gained[131:132, :] = jnp.sum(jnp.where(below, 0.0, ends), axis=0, keepdims=True)
    second = last[PACKED : PACKED + 40] * cells[half, 0:40, :]
    gained[98:99, :] = jnp.sum(second, axis=0, keepdims=True)
    lost = jnp.dot(table16[...], cells16[half], preferred_element_type=F32)
    for pos in range(4):
        b = (4 * half + pos + 6) % 8
        col = slice(pos * LANES, (pos + 1) * LANES)
        share = cloudy[b]
        for row in range(0, ROWS, 8):
            rows = slice(row, row + 8)
            change = gained[rows, col] - cells[half, rows, col] * lost[rows, col]
            change = change.astype(BF16).astype(F32) * share
            put(b, row, moved[b, rows, :] + change)


def kernel(
    state, cx, cy, order, count, gain, loss, out,
    wide, moved, cells, cells16, stacked, chooser, matrix, corner, corner16, square, table, table16,
    gained, weights, cloudy, xs, ys, xr, yr, send_sem, recv_sem,
):
    gx, gy = lax.axis_index("gx"), lax.axis_index("gy")
    nx, ny = lax.axis_size("gx"), lax.axis_size("gy")
    peers = (
        (lax.rem(gx + nx - 1, nx), gy),
        (lax.rem(gx + 1, nx), gy),
        (gx, lax.rem(gy + ny - 1, ny)),
        (gx, lax.rem(gy + 1, ny)),
    )
    barrier = pltpu.get_barrier_semaphore()
    for peer in peers:
        pl.semaphore_signal(barrier, inc=1, device_id=peer, device_id_type=MESH)

    def copy(step, side):
        sent, kept = (xs, xr) if side < 2 else (ys, yr)
        return pltpu.make_async_remote_copy(
            src_ref=sent.at[step, side % 2],
            dst_ref=kept.at[step, side % 2],
            send_sem=send_sem.at[step, side],
            recv_sem=recv_sem.at[step, side],
            device_id=peers[side],
            device_id_type=MESH,
        )

    def pack_x(step, side):
        for column in range(2):
            xs[step, side, column, 0:ROWS, :] = wide[2 + 6 * side + column].astype(BF16)

    for b in range(CX):
        for row in range(0, COMPS, 8):
            n = min(8, COMPS - row)
            wide[b + 2, row : row + n, :] = state[pl.ds(row * CX + b, n, stride=CX), :]
        wide[b + 2, COMPS:ROWS, :] = jnp.zeros((ROWS - COMPS, LANES), F32)
    for side in range(2):
        for step in range(2):
            for column in range(2):
                xs[step, side, column, ROWS - 8 :, :] = jnp.zeros((PACKED - ROWS + 8, LANES), BF16)
        pack_x(0, side)
    pack_y(wide, ys.at[0])
    pl.semaphore_wait(barrier, 4)
    for side in range(4):
        copy(0, side).start()

    cells[...] = jnp.zeros_like(cells)
    cells16[...] = jnp.zeros_like(cells16)
    gained[0:40, :] = jnp.zeros((40, HALF), F32)
    gained[ROWS - 8 :, :] = jnp.zeros((8, HALF), F32)
    for b in range(CX):
        found = jnp.int32(0)
        for k in range(CX):
            hit = (order[0, 0, k] == b) & (k < count[0, 0])
            found = found + hit.astype(jnp.int32)
        cloudy[b] = found.astype(F32)
    build_weights(cx, cy, weights)
    stack_gain(gain, stacked)
    exchange(stacked, chooser)
    build_gain(stacked, matrix, corner, corner.at[PACKED : PACKED + 48, 0:LANES])
    build_loss(loss, square, table)
    corner16[...] = corner[...].astype(BF16)
    table16[...] = table[...].astype(BF16)

    for step in range(2):
        for side in range(4):
            copy(step, side).wait_recv()
        for column in range(2):
            wide[column] = xr[step, 1, column, 0:ROWS, :].astype(F32)
            wide[CX + 2 + column] = xr[step, 0, column, 0:ROWS, :].astype(F32)
        transport(wide, yr.at[step, 1], yr.at[step, 0], weights, moved, cells, cells16)

        def put(b, row, value):
            if step == 0:
                wide[b + 2, row : row + 8, :] = value
            else:
                n = min(8, COMPS - row)
                out[pl.ds(row * CX + b, n, stride=CX), :] = value[0:n]

        for half in range(2):
            collide(half, matrix, corner16, table16, moved, cells, cells16, gained, cloudy, put)
            if step == 0 and half == 0:
                for side in range(2):
                    pack_x(1, side)
                for side in range(2):
                    copy(1, side).start()
        if step == 0:
            pack_y(wide, ys.at[1])
            for side in range(2, 4):
                copy(1, side).start()
    for step in range(2):
        for side in range(4):
            copy(step, side).wait_send()


def per_device(bin_state, courant_x, courant_y, cloudy_order, block_count, gain_kernel, loss_rate):
    vmem = pl.BlockSpec(memory_space=pltpu.VMEM)
    smem = pl.BlockSpec(memory_space=pltpu.SMEM)
    flat = bin_state.reshape(COMPS * CX, LANES)
    result = pl.pallas_call(
        kernel,
        out_shape=jax.ShapeDtypeStruct(flat.shape, F32),
        in_specs=[vmem, vmem, vmem, smem, smem, vmem, vmem],
        out_specs=vmem,
        scratch_shapes=[
            pltpu.VMEM((CX + 4, ROWS, LANES), F32),
            pltpu.VMEM((CX, ROWS, LANES), F32),
            pltpu.VMEM((2, 152, HALF), F32),
            pltpu.VMEM((2, 256, HALF), BF16),
            pltpu.VMEM((480, WIDE), BF16),
            pltpu.VMEM((WIDE, 384), BF16),
            pltpu.VMEM((len(GROUPS) * SLAB, 256), BF16),
            pltpu.VMEM((PACKED + 48, 256), F32),
            pltpu.VMEM((PACKED + 48, 256), BF16),
            pltpu.VMEM((LANES, LANES), F32),
            pltpu.VMEM((PACKED, 256), F32),
            pltpu.VMEM((PACKED, 256), BF16),
            pltpu.VMEM((ROWS, HALF), F32),
            pltpu.VMEM((9, CX, LANES), F32),
            pltpu.SMEM((CX,), F32),
            pltpu.VMEM((2, 2, 2, PACKED, LANES), BF16),
            pltpu.VMEM((2, 2, PACKED, LANES), BF16),
            pltpu.VMEM((2, 2, 2, PACKED, LANES), BF16),
            pltpu.VMEM((2, 2, PACKED, LANES), BF16),
            pltpu.SemaphoreType.DMA((2, 4)),
            pltpu.SemaphoreType.DMA((2, 4)),
        ],
        compiler_params=pltpu.CompilerParams(collective_id=0, has_side_effects=True),
        name="microphysics",
    )(flat, courant_x, courant_y, cloudy_order, block_count, gain_kernel, loss_rate)
    return result.reshape(bin_state.shape)


def solution(mesh):
    placed = (
        P(None, "gx", "gy"),
        P("gx", "gy"),
        P("gx", "gy"),
        P("gx", "gy", None),
        P("gy", "gx"),
        P(),
        P(),
    )
    return jax.shard_map(
        per_device, mesh=mesh, in_specs=placed, out_specs=P(None, "gx", "gy"), check_vma=False
    )
```

time: 203 us -> 34.7 us (0.17); the launches traced: 200 us -> 34.5 us
  local copies, waits for them, and re-layouts: 85.8 us -> 1.88 us
  matrix products: 53.3 us -> 0 us
  Pallas kernels: 0 us -> 31.9 us
  starting transfers between devices: 27.8 us -> 0 us
  other arithmetic: 24.7 us -> 0 us
  waiting for transfers between devices: 7.05 us -> 0 us
    mul x20 -> x0, local copies, waits for them, and re-layouts: 84.9 us -> none  [collide(): former_bins[:, None, :] * latter_bins[None, :, :]]
    dot_general x60 -> x0, matrix products: 53.3 us -> none  [the longest x20 44.6 us: collide(): jnp.dot(gain_kernel[pair_index], product, preferred_element_type=jnp.floa...]
    pallas_call x0 -> x1, Pallas kernels: none -> 31.9 us  [per_device(): pl.pallas_call(kernel, out_shape=jax.ShapeDtypeStruct(flat.shape, F32), i...]
    ppermute x8 -> x0, starting transfers between devices: 27.8 us -> none  [the longest x4 23.8 us: with_halo(): after = lax.ppermute(leading, axis, down)]
    mul x2 -> x0, other arithmetic: 16.4 us -> none  [collide(): former_bins[:, None, :] * latter_bins[None, :, :]]
    ppermute x8 -> x0, waiting for transfers between devices: 7.05 us -> none  [the longest x4 7.04 us: with_halo(): before = lax.ppermute(last, axis, up)]
    convert_element_type x8 -> x0, other arithmetic: 5.95 us -> none  [the longest x2 3.5 us: per_device(): bin_values = state_now.astype(jnp.bfloat16)]
  transfers between devices with their start and end apart: 8 -> 0, of which waited for: 3 -> 0; matrix products, arithmetic and copies ran while one was open for 1% -> 0% of each run, Pallas kernels for 0% -> 0%
where the time goes in v1:
time: 34.7 us; the launch traced here: 34.5 us
  Pallas kernels  31.9 us (92%)
  local copies, waits for them, and re-layouts  1.88 us (5%)
  between operations  0.66 us (2%)
    pallas_call x1, Pallas kernels, per_device(): pl.pallas_call(kernel, out_shape=jax.ShapeDtypeStruct(flat.shape, F32), i...  31.9 us
    unnamed x1, local copies, waits for them, and re-layouts  1.88 us

profile of v1, /device:TPU:2, one launch (start us, length us, event | category | flops | bytes accessed | tf_op | source)
XLA Modules:
  0.0 34.5 jit_solution(15600143871337294392)
XLA Ops:
  0.7 31.9 %microphysics.1 = f32[1056,128]{1,0:T(8,128)} custom-call(f32[1056,128]{1,0:T(8,128)} %bitcast.3, f32[8,128]{1,0:T(8,128)} %cx.1, f32[8,128]{1,0:T(8,128)} %cy.1, s32[1,1,8]{2,1,0:T(1,128)} %order.1, s32[1,1]{1,0:T(1,128)S(6)} %copy.9.count, bf16[10,33,1089]{2,1,0:T(8,128)(2,1)} %gain.1, bf16[10,33,33]{2,1,0:T(8,128)(2,1)} %loss.1), custom_call_target="tpu_custom_call" | custom-call | tf_op jit(solution)/shard_map/microphysics/pallas_call | solution.py:322
  32.6 1.9 %copy.10 = f32[132,8,128]{2,1,0:T(8,128)} copy(f32[132,8,128]{2,1,0:T(8,128)} %bitcast.2) | data formatting | bytes 1081344

commit v2 on v1

--- a/solution.py
+++ b/solution.py
@@ -131,56 +131,60 @@
     weights[8] = own
 
 
-def pack_y(wide, ys):
-    ys[...] = jnp.zeros_like(ys)
-    for row in range(0, ROWS, 16):
-        n = min(16, ROWS - row)
-        lane = iota((n, LANES), 1)
-        left = jnp.zeros((n, LANES), F32)
-        right = jnp.zeros((n, LANES), F32)
+def build_bands(weights, bands):
+    def block(b, carry):
+        row, lane = iota((LANES, LANES), 0), iota((LANES, LANES), 1)
+        left, right = row - 8 * b, row - 64 - 8 * b
+        far = jnp.full_like(row, -1000)
+        outer = jnp.where((left >= 0) & (left < 8), left - 8, far)
+        outer = jnp.where((right >= 0) & (right < 8), right + LANES, outer)
+        for part, place in ((0, row), (1, outer)):
+            value = jnp.zeros((LANES, LANES), F32)
+            for k, shift in ((4, LEV), (5, 2 * LEV), (6, -LEV), (7, -2 * LEV)):
+                value = jnp.where(place - lane == shift, -weights[k, pl.ds(b, 1), :], value)
+            bands[b, part * LANES : (part + 1) * LANES, :] = value.astype(BF16)
+        return carry
+
+    lax.fori_loop(0, CX, block, 0)
+
+
+def pack_y(narrow, ys):
+    lane = iota((16, LANES), 1)
+    for row in range(0, PACKED, 16):
+        left = jnp.zeros((16, LANES), BF16)
+        right = jnp.zeros((16, LANES), BF16)
         for b in range(CX):
-            value = wide[b + 2, row : row + n, :]
-            inside = (lane >= 8 * b) & (lane < 8 * b + 8)
-            left = jnp.where(inside, pltpu.roll(value, 8 * b, 1) if b else value, left)
-            right = jnp.where(inside, pltpu.roll(value, (8 * b + 8) % LANES, 1), right)
-        ys[0, row : row + n, :] = left.astype(BF16)
-        ys[1, row : row + n, :] = right.astype(BF16)
-
-
-def transport(wide, left, right, weights, moved, cells, cells16):
-    def block(pos, carry):
+            value = narrow[b, row : row + 16, 0:LANES]
+            at = 64 + 8 * b
+            left = jnp.where((lane >= at) & (lane < at + 8), pltpu.roll(value, at, 1), left)
+            at = 8 * b
+            right = jnp.where((lane >= at) & (lane < at + 8), pltpu.roll(value, at + 8, 1), right)
+        ys[0, row : row + 16, :] = left
+        ys[1, row : row + 16, :] = right
+
+
+def transport(wide, narrow, bands, weights, moved, cells, cells16):
+    for pos in range(CX):
         b = (pos + 6) % 8
-        half, col = pos // 4, pl.multiple_of((pos % 4) * LANES, LANES)
-        w = [weights[k, pl.ds(b, 1), :] for k in range(9)]
-        back = (120 - 8 * b) % LANES
-        fore = (LANES - 8 * b) % LANES
+        half, cols = pos // 4, slice((pos % 4) * LANES, (pos % 4 + 1) * LANES)
+        w = [weights[k, b : b + 1, :] for k in (0, 1, 2, 3, 8)]
+        flux = jnp.dot(narrow[b], bands[b], preferred_element_type=F32)
         for row in range(0, ROWS, 16):
             n = min(16, ROWS - row)
-            lane = iota((n, LANES), 1)
             rows = slice(row, row + n)
-            q = wide[b + 2, rows, :]
-            total = w[8] * q
+            total = w[4] * wide[b + 2, rows, :] + flux[rows]
             total = total - w[0] * wide[b + 3, rows, :] - w[1] * wide[b + 4, rows, :]
             total = total - w[2] * wide[b + 1, rows, :] - w[3] * wide[b, rows, :]
-            before = pltpu.roll(left[rows, :].astype(F32), back, 1)
-            after = pltpu.roll(right[rows, :].astype(F32), fore, 1)
-            total = total - w[4] * pltpu.roll(jnp.where(lane < LEV, after, q), LANES - LEV, 1)
-            total = total - w[5] * pltpu.roll(jnp.where(lane < 2 * LEV, after, q), LANES - 2 * LEV, 1)
-            total = total - w[6] * pltpu.roll(jnp.where(lane >= LANES - LEV, before, q), LEV, 1)
-            total = total - w[7] * pltpu.roll(jnp.where(lane >= LANES - 2 * LEV, before, q), 2 * LEV, 1)
             total = jnp.maximum(total, 0.0)
             moved[b, rows, :] = total
             rounded = total.astype(BF16)
-            cells[half, rows, pl.ds(col, LANES)] = rounded.astype(F32)
+            cells[half, rows, cols] = rounded.astype(F32)
             if row < 96:
-                cells16[half, rows, pl.ds(col, LANES)] = rounded
+                cells16[half, rows, cols] = rounded
             elif row == 96:
                 kept = jnp.where(iota((n, LANES), 0) < 3, total, 0.0)
-                cells16[half, rows, pl.ds(col, LANES)] = kept.astype(BF16)
-        cells16[half, 128:176, pl.ds(col, LANES)] = cells[half, 99:147, pl.ds(col, LANES)].astype(BF16)
-        return carry
-
-    lax.fori_loop(0, CX, block, 0)
+                cells16[half, rows, cols] = kept.astype(BF16)
+        cells16[half, 128:176, cols] = cells[half, 99:147, cols].astype(BF16)
 
 
 def collide(half, matrix, corner16, table16, moved, cells, cells16, gained, cloudy, put):
@@ -212,17 +216,18 @@
         b = (4 * half + pos + 6) % 8
         col = slice(pos * LANES, (pos + 1) * LANES)
         share = cloudy[b]
-        for row in range(0, ROWS, 8):
-            rows = slice(row, row + 8)
+        for row in range(0, ROWS, 16):
+            rows = slice(row, min(row + 16, ROWS))
             change = gained[rows, col] - cells[half, rows, col] * lost[rows, col]
             change = change.astype(BF16).astype(F32) * share
             put(b, row, moved[b, rows, :] + change)
 
 
 def kernel(
-    state, cx, cy, order, count, gain, loss, out,
-    wide, moved, cells, cells16, stacked, chooser, matrix, corner, corner16, square, table, table16,
-    gained, weights, cloudy, xs, ys, xr, yr, send_sem, recv_sem,
+    state_hbm, cx_hbm, cy_hbm, order_hbm, count, gain_hbm, loss_hbm, out,
+    state, cx, cy, order, gain, loss,
+    wide, narrow, moved, cells, cells16, stacked, chooser, matrix, corner, corner16, square, table, table16,
+    gained, weights, bands, cloudy, xs, ys, xr, yr, load_sem, send_sem, recv_sem,
 ):
     gx, gy = lax.axis_index("gx"), lax.axis_index("gy")
     nx, ny = lax.axis_size("gx"), lax.axis_size("gy")
@@ -232,6 +237,17 @@
         (gx, lax.rem(gy + ny - 1, ny)),
         (gx, lax.rem(gy + 1, ny)),
     )
+    loads = [
+        pltpu.make_async_copy(source, kept, load_sem.at[k])
+        for k, (source, kept) in enumerate(
+            (
+                (state_hbm, state), (cx_hbm, cx), (cy_hbm, cy), (order_hbm, order),
+                (gain_hbm, gain), (loss_hbm, loss),
+            )
+        )
+    ]
+    for load in loads:
+        load.start()
     barrier = pltpu.get_barrier_semaphore()
     for peer in peers:
         pl.semaphore_signal(barrier, inc=1, device_id=peer, device_id_type=MESH)
@@ -247,29 +263,35 @@
             device_id_type=MESH,
         )
 
-    def pack_x(step, side):
-        for column in range(2):
-            xs[step, side, column, 0:ROWS, :] = wide[2 + 6 * side + column].astype(BF16)
+    def pack_x(step):
+        for side in range(2):
+            for column in range(2):
+                xs[step, side, column] = narrow[6 * side + column, :, 0:LANES]
 
     for b in range(CX):
-        for row in range(0, COMPS, 8):
-            n = min(8, COMPS - row)
-            wide[b + 2, row : row + n, :] = state[pl.ds(row * CX + b, n, stride=CX), :]
-        wide[b + 2, COMPS:ROWS, :] = jnp.zeros((ROWS - COMPS, LANES), F32)
-    for side in range(2):
-        for step in range(2):
-            for column in range(2):
-                xs[step, side, column, ROWS - 8 :, :] = jnp.zeros((PACKED - ROWS + 8, LANES), BF16)
-        pack_x(0, side)
-    pack_y(wide, ys.at[0])
+        wide[b + 2, 128:ROWS, :] = jnp.zeros((ROWS - 128, LANES), F32)
+        narrow[b, 128:PACKED, 0:LANES] = jnp.zeros((PACKED - 128, LANES), BF16)
+    loads[0].wait()
+    for b in range(CX):
+        for row in range(0, 128, 16):
+            value = state[pl.ds(row * CX + b, 16, stride=CX), :]
+            wide[b + 2, row : row + 16, :] = value
+            narrow[b, row : row + 16, 0:LANES] = value.astype(BF16)
+        value = state[pl.ds(128 * CX + b, COMPS - 128, stride=CX), :]
+        wide[b + 2, 128:COMPS, :] = value
+        narrow[b, 128:ROWS, 0:LANES] = wide[b + 2, 128:ROWS, :].astype(BF16)
+    pack_y(narrow, ys.at[0])
+    pack_x(0)
     pl.semaphore_wait(barrier, 4)
-    for side in range(4):
+    for side in (2, 3, 0, 1):
         copy(0, side).start()
 
     cells[...] = jnp.zeros_like(cells)
     cells16[...] = jnp.zeros_like(cells16)
     gained[0:40, :] = jnp.zeros((40, HALF), F32)
     gained[ROWS - 8 :, :] = jnp.zeros((8, HALF), F32)
+    for load in loads[1:]:
+        load.wait()
     for b in range(CX):
         found = jnp.int32(0)
         for k in range(CX):
@@ -277,6 +299,7 @@
             found = found + hit.astype(jnp.int32)
         cloudy[b] = found.astype(F32)
     build_weights(cx, cy, weights)
+    build_bands(weights, bands)
     stack_gain(gain, stacked)
     exchange(stacked, chooser)
     build_gain(stacked, matrix, corner, corner.at[PACKED : PACKED + 48, 0:LANES])
@@ -290,24 +313,28 @@
         for column in range(2):
             wide[column] = xr[step, 1, column, 0:ROWS, :].astype(F32)
             wide[CX + 2 + column] = xr[step, 0, column, 0:ROWS, :].astype(F32)
-        transport(wide, yr.at[step, 1], yr.at[step, 0], weights, moved, cells, cells16)
+        halo = yr[step, 0] + yr[step, 1]
+        for b in range(CX):
+            narrow[b, :, LANES : 2 * LANES] = halo
+        transport(wide, narrow, bands, weights, moved, cells, cells16)
 
         def put(b, row, value):
             if step == 0:
-                wide[b + 2, row : row + 8, :] = value
+                n = value.shape[0]
+                wide[b + 2, row : row + n, :] = value
+                narrow[b, row : row + n, 0:LANES] = value.astype(BF16)
             else:
-                n = min(8, COMPS - row)
+                n = min(16, COMPS - row)
                 out[pl.ds(row * CX + b, n, stride=CX), :] = value[0:n]
 
         for half in range(2):
             collide(half, matrix, corner16, table16, moved, cells, cells16, gained, cloudy, put)
             if step == 0 and half == 0:
-                for side in range(2):
-                    pack_x(1, side)
+                pack_x(1)
                 for side in range(2):
                     copy(1, side).start()
         if step == 0:
-            pack_y(wide, ys.at[1])
+            pack_y(narrow, ys.at[1])
             for side in range(2, 4):
                 copy(1, side).start()
     for step in range(2):
@@ -315,17 +342,28 @@
             copy(step, side).wait_send()
 
 
+def pinned(array):
+    return pltpu.with_memory_space_constraint(array, pltpu.HBM)
+
+
 def per_device(bin_state, courant_x, courant_y, cloudy_order, block_count, gain_kernel, loss_rate):
     vmem = pl.BlockSpec(memory_space=pltpu.VMEM)
-    smem = pl.BlockSpec(memory_space=pltpu.SMEM)
+    hbm = pl.BlockSpec(memory_space=pltpu.HBM)
     flat = bin_state.reshape(COMPS * CX, LANES)
     result = pl.pallas_call(
         kernel,
         out_shape=jax.ShapeDtypeStruct(flat.shape, F32),
-        in_specs=[vmem, vmem, vmem, smem, smem, vmem, vmem],
+        in_specs=[hbm] * 4 + [pl.BlockSpec(memory_space=pltpu.VMEM)] + [hbm] * 2,
         out_specs=vmem,
         scratch_shapes=[
+            pltpu.VMEM(flat.shape, F32),
+            pltpu.VMEM(courant_x.shape, F32),
+            pltpu.VMEM(courant_y.shape, F32),
+            pltpu.SMEM(cloudy_order.shape, jnp.int32),
+            pltpu.VMEM(gain_kernel.shape, BF16),
+            pltpu.VMEM(loss_rate.shape, BF16),
             pltpu.VMEM((CX + 4, ROWS, LANES), F32),
+            pltpu.VMEM((CX, PACKED, 2 * LANES), BF16),
             pltpu.VMEM((CX, ROWS, LANES), F32),
             pltpu.VMEM((2, 152, HALF), F32),
             pltpu.VMEM((2, 256, HALF), BF16),
@@ -339,17 +377,24 @@
             pltpu.VMEM((PACKED, 256), BF16),
             pltpu.VMEM((ROWS, HALF), F32),
             pltpu.VMEM((9, CX, LANES), F32),
+            pltpu.VMEM((CX, 2 * LANES, LANES), BF16),
             pltpu.SMEM((CX,), F32),
             pltpu.VMEM((2, 2, 2, PACKED, LANES), BF16),
             pltpu.VMEM((2, 2, PACKED, LANES), BF16),
             pltpu.VMEM((2, 2, 2, PACKED, LANES), BF16),
             pltpu.VMEM((2, 2, PACKED, LANES), BF16),
+            pltpu.SemaphoreType.DMA((6,)),
             pltpu.SemaphoreType.DMA((2, 4)),
             pltpu.SemaphoreType.DMA((2, 4)),
         ],
-        compiler_params=pltpu.CompilerParams(collective_id=0, has_side_effects=True),
+        compiler_params=pltpu.CompilerParams(
+            collective_id=0, has_side_effects=True, vmem_limit_bytes=24 * 1024 * 1024
+        ),
         name="microphysics",
-    )(flat, courant_x, courant_y, cloudy_order, block_count, gain_kernel, loss_rate)
+    )(
+        pinned(flat), pinned(courant_x), pinned(courant_y), pinned(cloudy_order), block_count,
+        pinned(gain_kernel), pinned(loss_rate),
+    )
     return result.reshape(bin_state.shape)
 
 

time: 34.7 us -> 28.4 us (0.82)
  Pallas kernels: 31.9 us -> 26.8 us
  local copies, waits for them, and re-layouts: 1.88 us -> 0.8 us
    pallas_call x1, Pallas kernels: 31.9 us -> 26.8 us  [per_device(): pl.pallas_call(kernel, out_shape=jax.ShapeDtypeStruct(flat.shape, F32), i...]
    unnamed x1, local copies, waits for them, and re-layouts: 1.88 us -> 0.8 us
where the time goes in v2:
time: 28.4 us; the launch traced here: 28.3 us
  Pallas kernels  26.8 us (94%)
  local copies, waits for them, and re-layouts  0.8 us (3%)
  between operations  0.66 us (2%)
    pallas_call x1, Pallas kernels, per_device(): pl.pallas_call(kernel, out_shape=jax.ShapeDtypeStruct(flat.shape, F32), i...  26.8 us
    unnamed x1, local copies, waits for them, and re-layouts  0.8 us

profile of v2, /device:TPU:2, one launch (start us, length us, event | category | flops | bytes accessed | tf_op | source)
XLA Modules:
  0.0 28.3 jit_solution(14021455111630689872)
XLA Ops:
  0.7 26.8 %microphysics.1 = f32[1056,128]{1,0:T(8,128)S(1)} custom-call(f32[1056,128]{1,0:T(8,128)} %bitcast.3, f32[8,128]{1,0:T(8,128)} %cx_hbm.1, f32[8,128]{1,0:T(8,128)} %cy_hbm.1, s32[1,1,8]{2,1,0:T(1,128)} %order_hbm.1, s32[1,1]{1,0:T(1,128)S(6)} %copy.9.count, bf16[10,33,1089]{2,1,0:T(8,128)(2,1)} %gain_hbm.1, bf16[10,33,33]{2,1,0:T(8,128)(2,1)} %loss_hbm.1), custom_call_target="tpu_custom_call" | custom-call | tf_op jit(solution)/shard_map/microphysics/pallas_call | solution.py:353
  27.5 0.8 %copy.10 = f32[132,8,128]{2,1,0:T(8,128)} copy(f32[132,8,128]{2,1,0:T(8,128)S(1)} %bitcast.2) | data formatting | bytes 1081344

commit v3 on v2

--- a/solution.py
+++ b/solution.py
@@ -33,6 +33,7 @@
 PAIR_OF = {(0, 0): 0, (0, 1): 1, (0, 2): 2, (0, 3): 3, (1, 1): 4, (1, 2): 5, (1, 3): 6, (2, 2): 7, (2, 3): 8, (3, 3): 9}
 CHUNK = 11
 SLAB = BINS * 32
+PARTS = ((0, 48), (48, 48), (96, 40))
 
 
 def iota(shape, dim):
@@ -62,7 +63,7 @@
         stacked[0:rows, part * width : (part + 1) * width] = parts[part]
 
 
-def window(stacked, pair, index, lane0):
+def window(stacked, lane, pair, index, lane0):
     row = PLACE[pair] * 48
     start = index * BINS
     tile, off = start // LANES, start % LANES
@@ -73,11 +74,13 @@
     first = moved(tile)
     if off + BINS <= LANES:
         return first
-    return jnp.where(iota((48, LANES), 1) < lane0 + LANES - off, first, moved(tile + 1))
+    return jnp.where(lane < lane0 + LANES - off, first, moved(tile + 1))
 
 
 def build_gain(stacked, matrix, corner, corner2):
     lane = iota((48, LANES), 1)
+    inside = {at % LANES: (lane >= at % LANES) & (lane < at % LANES + BINS) for at in OFFSET}
+    nothing = jnp.zeros((48, LANES), BF16)
     corner[...] = jnp.zeros_like(corner)
     corner2[...] = jnp.zeros_like(corner2)
     for group, (target, factor, pairs) in enumerate(GROUPS):
@@ -85,12 +88,11 @@
             low, high = None, None
             for pair, cls in sorted(pairs, key=lambda entry: entry[1]):
                 lane0 = OFFSET[cls] % LANES
-                piece = window(stacked, pair, index, lane0)
-                inside = (lane >= lane0) & (lane < lane0 + BINS)
+                piece = window(stacked, lane, pair, index, lane0)
                 if cls == 3:
-                    high = jnp.where(inside, piece, jnp.zeros_like(piece))
+                    high = jnp.where(inside[lane0], piece, nothing)
                 else:
-                    low = jnp.where(inside, piece, jnp.zeros_like(piece) if low is None else low)
+                    low = jnp.where(inside[lane0], piece, nothing if low is None else low)
             row = group * SLAB + index * 32
             for value, col in ((low, 0), (high, LANES)):
                 if value is None:
@@ -148,19 +150,30 @@
     lax.fori_loop(0, CX, block, 0)
 
 
-def pack_y(narrow, ys):
-    lane = iota((16, LANES), 1)
-    for row in range(0, PACKED, 16):
-        left = jnp.zeros((16, LANES), BF16)
-        right = jnp.zeros((16, LANES), BF16)
-        for b in range(CX):
-            value = narrow[b, row : row + 16, 0:LANES]
-            at = 64 + 8 * b
-            left = jnp.where((lane >= at) & (lane < at + 8), pltpu.roll(value, at, 1), left)
-            at = 8 * b
-            right = jnp.where((lane >= at) & (lane < at + 8), pltpu.roll(value, at + 8, 1), right)
-        ys[0, row : row + 16, :] = left
-        ys[1, row : row + 16, :] = right
+def edges(block, n, dtype):
+    lane = iota((n, LANES), 1)
+    total = jnp.zeros((n, LANES), dtype)
+    for b in range(CX):
+        value = block(b)
+        for at, shift in ((8 * b, 8 * b + 8), (64 + 8 * b, 64 + 8 * b)):
+            total = jnp.where((lane >= at) & (lane < at + 8), pltpu.roll(value, shift, 1), total)
+    return total
+
+
+def one_side(side, lane, total):
+    return jnp.where(lane >= 64 if side == 0 else lane < 64, total, jnp.zeros_like(total))
+
+
+def place(total, row, n, half, cells, cells16, cols):
+    rows = slice(row, row + n)
+    rounded = total.astype(BF16)
+    cells[half, rows, cols] = rounded.astype(F32)
+    if row < 96:
+        cells16[half, rows, cols] = rounded
+    else:
+        kept = jnp.where(iota((16, LANES), 0) < 3, total[0:16], 0.0)
+        cells16[half, 96:112, cols] = kept.astype(BF16)
+        cells16[half, 128:176, cols] = cells[half, 99:147, cols].astype(BF16)
 
 
 def transport(wide, narrow, bands, weights, moved, cells, cells16):
@@ -169,26 +182,25 @@
         half, cols = pos // 4, slice((pos % 4) * LANES, (pos % 4 + 1) * LANES)
         w = [weights[k, b : b + 1, :] for k in (0, 1, 2, 3, 8)]
         flux = jnp.dot(narrow[b], bands[b], preferred_element_type=F32)
-        for row in range(0, ROWS, 16):
-            n = min(16, ROWS - row)
+        for row, n in PARTS:
             rows = slice(row, row + n)
             total = w[4] * wide[b + 2, rows, :] + flux[rows]
             total = total - w[0] * wide[b + 3, rows, :] - w[1] * wide[b + 4, rows, :]
             total = total - w[2] * wide[b + 1, rows, :] - w[3] * wide[b, rows, :]
             total = jnp.maximum(total, 0.0)
             moved[b, rows, :] = total
-            rounded = total.astype(BF16)
-            cells[half, rows, cols] = rounded.astype(F32)
-            if row < 96:
-                cells16[half, rows, cols] = rounded
-            elif row == 96:
-                kept = jnp.where(iota((n, LANES), 0) < 3, total, 0.0)
-                cells16[half, rows, cols] = kept.astype(BF16)
-        cells16[half, 128:176, cols] = cells[half, 99:147, cols].astype(BF16)
-
-
-def collide(half, matrix, corner16, table16, moved, cells, cells16, gained, cloudy, put):
-    total = {}
+            place(total, row, n, half, cells, cells16, cols)
+
+
+def gather_edges(moved, edge, cells, cells16):
+    for row, n in PARTS:
+        total = edges(lambda b: moved[b, row : row + n, :], n, F32)
+        edge[row : row + n, :] = total
+        place(total, row, n, 0, cells, cells16, slice(0, LANES))
+
+
+def collide(half, matrix, corner16, table16, cells, cells16, gained, finish):
+    total, width = {}, cells.shape[2]
     for group, (target, factor, pairs) in enumerate(GROUPS):
         depth = 256 if any(cls == 3 for _, cls in pairs) else 128
         for first in range(0, BINS, CHUNK):
@@ -206,28 +218,25 @@
         gained[target * BINS : target * BINS + 32, :] = total[target]
     last = jnp.dot(corner16[...], cells16[half], preferred_element_type=F32)
     ends = last[0:ROWS] * cells[half, 0:ROWS, :]
-    below = iota((ROWS, HALF), 0) < 2 * BINS
+    below = iota((ROWS, width), 0) < 2 * BINS
     gained[65:66, :] = jnp.sum(jnp.where(below, ends, 0.0), axis=0, keepdims=True)
     gained[131:132, :] = jnp.sum(jnp.where(below, 0.0, ends), axis=0, keepdims=True)
     second = last[PACKED : PACKED + 40] * cells[half, 0:40, :]
     gained[98:99, :] = jnp.sum(second, axis=0, keepdims=True)
     lost = jnp.dot(table16[...], cells16[half], preferred_element_type=F32)
-    for pos in range(4):
-        b = (4 * half + pos + 6) % 8
+    for pos in range(width // LANES):
         col = slice(pos * LANES, (pos + 1) * LANES)
-        share = cloudy[b]
-        for row in range(0, ROWS, 16):
-            rows = slice(row, min(row + 16, ROWS))
+        for row, n in PARTS:
+            rows = slice(row, row + n)
             change = gained[rows, col] - cells[half, rows, col] * lost[rows, col]
-            change = change.astype(BF16).astype(F32) * share
-            put(b, row, moved[b, rows, :] + change)
+            finish(pos, row, change.astype(BF16).astype(F32))
 
 
 def kernel(
     state_hbm, cx_hbm, cy_hbm, order_hbm, count, gain_hbm, loss_hbm, out,
     state, cx, cy, order, gain, loss,
     wide, narrow, moved, cells, cells16, stacked, chooser, matrix, corner, corner16, square, table, table16,
-    gained, weights, bands, cloudy, xs, ys, xr, yr, load_sem, send_sem, recv_sem,
+    gained, weights, bands, cloudy, share, edge, edge_cells, edge_cells16, edge_gained, xs, ys, xr, yr, load_sem, send_sem, recv_sem,
 ):
     gx, gy = lax.axis_index("gx"), lax.axis_index("gy")
     nx, ny = lax.axis_size("gx"), lax.axis_size("gy")
@@ -280,7 +289,13 @@
         value = state[pl.ds(128 * CX + b, COMPS - 128, stride=CX), :]
         wide[b + 2, 128:COMPS, :] = value
         narrow[b, 128:ROWS, 0:LANES] = wide[b + 2, 128:ROWS, :].astype(BF16)
-    pack_y(narrow, ys.at[0])
+    lane = iota((48, LANES), 1)
+    for row in range(0, PACKED, 48):
+        total = edges(lambda b: narrow[b, row : row + 48, 0:LANES], 48, BF16)
+        for side in range(2):
+            ys[0, side, row : row + 48, :] = one_side(side, lane, total)
+    for side in range(2):
+        ys[1, side, 128:PACKED, :] = jnp.zeros((PACKED - 128, LANES), BF16)
     pack_x(0)
     pl.semaphore_wait(barrier, 4)
     for side in (2, 3, 0, 1):
@@ -288,7 +303,11 @@
 
     cells[...] = jnp.zeros_like(cells)
     cells16[...] = jnp.zeros_like(cells16)
+    edge_cells[...] = jnp.zeros_like(edge_cells)
+    edge_cells16[...] = jnp.zeros_like(edge_cells16)
     gained[0:40, :] = jnp.zeros((40, HALF), F32)
+    edge_gained[0:40, :] = jnp.zeros((40, LANES), F32)
+    edge_gained[ROWS - 8 :, :] = jnp.zeros((8, LANES), F32)
     gained[ROWS - 8 :, :] = jnp.zeros((8, HALF), F32)
     for load in loads[1:]:
         load.wait()
@@ -298,6 +317,12 @@
             hit = (order[0, 0, k] == b) & (k < count[0, 0])
             found = found + hit.astype(jnp.int32)
         cloudy[b] = found.astype(F32)
+    lane = iota((8, LANES), 1)
+    shares = jnp.zeros((8, LANES), F32)
+    for b in range(CX):
+        for at in (8 * b, 64 + 8 * b):
+            shares = shares + jnp.where((lane >= at) & (lane < at + 8), 1.0, 0.0) * cloudy[b]
+    share[...] = shares
     build_weights(cx, cy, weights)
     build_bands(weights, bands)
     stack_gain(gain, stacked)
@@ -318,25 +343,45 @@
             narrow[b, :, LANES : 2 * LANES] = halo
         transport(wide, narrow, bands, weights, moved, cells, cells16)
 
-        def put(b, row, value):
-            if step == 0:
-                n = value.shape[0]
-                wide[b + 2, row : row + n, :] = value
-                narrow[b, row : row + n, 0:LANES] = value.astype(BF16)
-            else:
-                n = min(16, COMPS - row)
-                out[pl.ds(row * CX + b, n, stride=CX), :] = value[0:n]
-
-        for half in range(2):
-            collide(half, matrix, corner16, table16, moved, cells, cells16, gained, cloudy, put)
-            if step == 0 and half == 0:
-                pack_x(1)
+        if step == 0:
+            gather_edges(moved, edge, edge_cells, edge_cells16)
+
+            def finish_edge(pos, row, change):
+                n = change.shape[0]
+                value = edge[row : row + n, :] + change * share[0:1, :]
+                value, lane = value.astype(BF16), iota((n, LANES), 1)
                 for side in range(2):
-                    copy(1, side).start()
-        if step == 0:
-            pack_y(narrow, ys.at[1])
+                    ys[1, side, row : row + n, :] = one_side(side, lane, value)
+
+            collide(
+                0, matrix, corner16, table16, edge_cells, edge_cells16, edge_gained, finish_edge
+            )
             for side in range(2, 4):
                 copy(1, side).start()
+
+        def collide_half(half):
+            def finish(pos, row, change):
+                b = (4 * half + pos + 6) % 8
+                n = change.shape[0]
+                value = moved[b, row : row + n, :] + change * cloudy[b]
+                if step == 0:
+                    wide[b + 2, row : row + n, :] = value
+                    narrow[b, row : row + n, 0:LANES] = value.astype(BF16)
+                else:
+                    n = min(n, COMPS - row)
+                    out[pl.ds(row * CX + b, n, stride=CX), :] = value[0:n]
+
+            collide(half, matrix, corner16, table16, cells, cells16, gained, finish)
+
+        if step == 0:
+            collide_half(0)
+            pack_x(1)
+            for side in range(2):
+                copy(1, side).start()
+            collide_half(1)
+        else:
+            collide_half(0)
+            collide_half(1)
     for step in range(2):
         for side in range(4):
             copy(step, side).wait_send()
@@ -379,6 +424,11 @@
             pltpu.VMEM((9, CX, LANES), F32),
             pltpu.VMEM((CX, 2 * LANES, LANES), BF16),
             pltpu.SMEM((CX,), F32),
+            pltpu.VMEM((8, LANES), F32),
+            pltpu.VMEM((ROWS, LANES), F32),
+            pltpu.VMEM((1, 152, LANES), F32),
+            pltpu.VMEM((1, 2 * LANES, LANES), BF16),
+            pltpu.VMEM((ROWS, LANES), F32),
             pltpu.VMEM((2, 2, 2, PACKED, LANES), BF16),
             pltpu.VMEM((2, 2, PACKED, LANES), BF16),
             pltpu.VMEM((2, 2, 2, PACKED, LANES), BF16),

time: 28.4 us -> 27.3 us (0.961)
  the two profiles are of different devices: /device:TPU:2 before, /device:TPU:1 now
where the time goes in v3:
time: 27.3 us; the launch traced here: 27.2 us
  Pallas kernels  25.7 us (94%)
  local copies, waits for them, and re-layouts  0.8 us (3%)
  between operations  0.66 us (2%)
    pallas_call x1, Pallas kernels, per_device(): pl.pallas_call(kernel, out_shape=jax.ShapeDtypeStruct(flat.shape, F32), i...  25.7 us
    unnamed x1, local copies, waits for them, and re-layouts  0.8 us

profile of v3, /device:TPU:1, one launch (start us, length us, event | category | flops | bytes accessed | tf_op | source)
XLA Modules:
  0.0 27.2 jit_solution(13699000269781170516)
XLA Ops:
  0.7 25.7 %microphysics.1 = f32[1056,128]{1,0:T(8,128)S(1)} custom-call(f32[1056,128]{1,0:T(8,128)} %bitcast.3, f32[8,128]{1,0:T(8,128)} %cx_hbm.1, f32[8,128]{1,0:T(8,128)} %cy_hbm.1, s32[1,1,8]{2,1,0:T(1,128)} %order_hbm.1, s32[1,1]{1,0:T(1,128)S(6)} %copy.9.count, bf16[10,33,1089]{2,1,0:T(8,128)(2,1)} %gain_hbm.1, bf16[10,33,33]{2,1,0:T(8,128)(2,1)} %loss_hbm.1), custom_call_target="tpu_custom_call" | custom-call | tf_op jit(solution)/shard_map/microphysics/pallas_call | solution.py:398
  26.4 0.8 %copy.10 = f32[132,8,128]{2,1,0:T(8,128)} copy(f32[132,8,128]{2,1,0:T(8,128)S(1)} %bitcast.2) | data formatting | bytes 1081344

commit v4 on v3

--- a/solution.py
+++ b/solution.py
@@ -176,8 +176,8 @@
         cells16[half, 128:176, cols] = cells[half, 99:147, cols].astype(BF16)
 
 
-def transport(wide, narrow, bands, weights, moved, cells, cells16):
-    for pos in range(CX):
+def transport(places, wide, narrow, bands, weights, moved, cells, cells16):
+    for pos in places:
         b = (pos + 6) % 8
         half, cols = pos // 4, slice((pos % 4) * LANES, (pos % 4 + 1) * LANES)
         w = [weights[k, b : b + 1, :] for k in (0, 1, 2, 3, 8)]
@@ -333,16 +333,26 @@
     table16[...] = table[...].astype(BF16)
 
     for step in range(2):
-        for side in range(4):
+
+        def columns_arrive():
+            for side in range(2):
+                copy(step, side).wait_recv()
+            for column in range(2):
+                wide[column] = xr[step, 1, column, 0:ROWS, :].astype(F32)
+                wide[CX + 2 + column] = xr[step, 0, column, 0:ROWS, :].astype(F32)
+
+        def move(places):
+            transport(places, wide, narrow, bands, weights, moved, cells, cells16)
+
+        if step == 0:
+            columns_arrive()
+        for side in range(2, 4):
             copy(step, side).wait_recv()
-        for column in range(2):
-            wide[column] = xr[step, 1, column, 0:ROWS, :].astype(F32)
-            wide[CX + 2 + column] = xr[step, 0, column, 0:ROWS, :].astype(F32)
         halo = yr[step, 0] + yr[step, 1]
         for b in range(CX):
             narrow[b, :, LANES : 2 * LANES] = halo
-        transport(wide, narrow, bands, weights, moved, cells, cells16)
-
+        if step == 0:
+            move(range(CX))
         if step == 0:
             gather_edges(moved, edge, edge_cells, edge_cells16)
 
@@ -380,8 +390,11 @@
                 copy(1, side).start()
             collide_half(1)
         else:
+            move(range(4, CX))
+            collide_half(1)
+            columns_arrive()
+            move(range(4))
             collide_half(0)
-            collide_half(1)
     for step in range(2):
         for side in range(4):
             copy(step, side).wait_send()

time: 27.3 us -> 26.2 us (0.960)
  the two profiles are of different devices: /device:TPU:1 before, /device:TPU:2 now
where the time goes in v4:
time: 26.2 us; the launch traced here: 26 us
  Pallas kernels  24.6 us (94%)
  local copies, waits for them, and re-layouts  0.8 us (3%)
  between operations  0.66 us (3%)
    pallas_call x1, Pallas kernels, per_device(): pl.pallas_call(kernel, out_shape=jax.ShapeDtypeStruct(flat.shape, F32), i...  24.6 us
    unnamed x1, local copies, waits for them, and re-layouts  0.8 us

profile of v4, /device:TPU:2, one launch (start us, length us, event | category | flops | bytes accessed | tf_op | source)
XLA Modules:
  0.0 26.0 jit_solution(13364495859630338789)
XLA Ops:
  0.7 24.6 %microphysics.1 = f32[1056,128]{1,0:T(8,128)S(1)} custom-call(f32[1056,128]{1,0:T(8,128)} %bitcast.3, f32[8,128]{1,0:T(8,128)} %cx_hbm.1, f32[8,128]{1,0:T(8,128)} %cy_hbm.1, s32[1,1,8]{2,1,0:T(1,128)} %order_hbm.1, s32[1,1]{1,0:T(1,128)S(6)} %copy.9.count, bf16[10,33,1089]{2,1,0:T(8,128)(2,1)} %gain_hbm.1, bf16[10,33,33]{2,1,0:T(8,128)(2,1)} %loss_hbm.1), custom_call_target="tpu_custom_call" | custom-call | tf_op jit(solution)/shard_map/microphysics/pallas_call | solution.py:411
  25.2 0.8 %copy.10 = f32[132,8,128]{2,1,0:T(8,128)} copy(f32[132,8,128]{2,1,0:T(8,128)S(1)} %bitcast.2) | data formatting | bytes 1081344
